TPU v7x, 16 devices: a whole 2x2x2 slice. The times are simulated.
16 devices in a mesh: tp: 2 (over z), side: 2 (over y), rep: 4 (over x, core).
Axes of the slice: x: 2, y: 2, z: 2, core: 2. Of those that a mesh axis runs over, the one named last changes fastest.
Arguments:
- w_up: float32 [2, 6, 896, 4864], P('side', None, ('rep', 'tp'))
- w_down: float32 [2, 6, 4864, 896], P('side', None, None, ('rep', 'tp'))
- g_up: float32 [2, 6, 896, 4864], P('side', None, ('rep', 'tp'))
- g_down: float32 [2, 6, 4864, 896], P('side', None, None, ('rep', 'tp'))
- learn_rate: float32 [2], P('side')
- prompts: bfloat16 [2, 4, 8192, 896], P('side', 'rep')
Outputs:
- output 1: float32 [2, 6, 896, 4864], P('side', None, ('rep', 'tp'))
- output 2: float32 [2, 6, 4864, 896], P('side', None, None, ('rep', 'tp'))
- output 3: bfloat16 [2, 4, 8192, 896], P('side', 'rep')
All inputs are finite; a program needn't handle non-finite values.
Results may differ from a plain program's by a relative error of at most 0.0155867.
Values are sent between devices in bfloat16 or wider.
A program may use at most 1 GiB of HBM per device.

v0:
```python
import jax
import jax.numpy as jnp
from jax import lax
from jax.experimental import pallas as pl
from jax.experimental.pallas import tpu as pltpu
from jax.sharding import PartitionSpec as P

MESH = pl.DeviceIdType.MESH
UNIT = 256
GROUP = 5
BLOCK = 512
PIECE = 128
EARLY = 2
LOAD_SLOTS = 4
STAGE_SLOTS = 36
RING = 32
N_LAG, D_LAG = 3, 6
RELAY_LAG = 4
FIRST_LATE = 3
MORE = 2
RELAYED = ((5, 2), (6, 2))
FRONTS = ((10, 15, 1, 40), (8, 14, 1, 44), (6, 13, 3, 24))
GELU_A = 0.7978845608028654
GELU_B = 0.7978845608028654 * 0.044715


def div(a, n):
    if isinstance(a, int):
        return a // n
    if n & (n - 1) == 0:
        return a >> (n.bit_length() - 1)
    return (a * ((1 << 16) // n + 1)) >> 16


def mod(a, n):
    return a - n * div(a, n)


def gelu(a):
    return a * (0.5 * jnp.tanh(a * (GELU_A + GELU_B * (a * a))) + 0.5)


def sync_kernel(
    rate_ref, w_up, w_dn, g_up, g_dn, prompts, out, nu, nd, wbuf, rin, rx,
    h, p, wv, fin, fnew, stage, rows_buf,
    ysem, rs, rlsem, sbsem, ss, lsem, stsem, fsem, tss, csem, iosem, psem, osem, rsem, hs, hr,
):
    layers, band, hidden = w_up.shape
    chunks = hidden // UNIT
    n_relay = sum(n for _, n in RELAYED)
    groups = -(-chunks // GROUP)
    lead = chunks - (groups - 1) * GROUP
    mid = EARLY * chunks
    gen = 2 * mid
    n_rows, d = out.shape
    my_rows = n_rows // 2
    blocks = my_rows // BLOCK
    pieces = BLOCK // PIECE

    tp = lax.axis_index("tp")
    side = lax.axis_index("side")
    rep = lax.axis_index("rep")
    x, k = rep // 2, rep % 2
    flip_tp = 1 - tp
    flip_rep = (1 - x) * 2 + k
    sib_rep = x * 2 + (1 - k)

    own, znb, xnb, dia = (x, tp), (x, flip_tp), (1 - x, tp), (1 - x, flip_tp)

    def both(c, b):
        return wbuf.at[c, :, b[0], k, b[1]]

    def core_half(c, core):
        return wbuf.at[c, :, :, core]

    def chunk_of(e):
        return e + jnp.where(e >= mid, mid, 0)

    def relayed(e):
        return ((mod(e, 6) == 5) & (e < mid)) | ((mod(e, 3) == 2) & (e >= mid + chunks))

    def by_z(e):
        return ((mod(div(e, 6) + mod(e, 6), 2) == 1) & (e < mid + chunks)) | ((mod(e, 3) == 1) & (e >= mid + chunks))

    def count(e0, e1, fn):
        return sum(1 for e in range(e0, e1) if fn(e))

    n_early = count(0, mid, relayed)

    def relay_index(e):
        return jnp.where(e < mid, div(e, 6), n_early + div(e - mid - chunks, 3))

    def zsem(e):
        return rs.at[0, mod(e, RING)]

    def xsem(e):
        return rs.at[1, mod(e, RING)]

    def dsem(e):
        return rs.at[2, mod(e, RING)]

    def sb_of(e):
        l = div(e, chunks)
        j = e - l * chunks
        g = jnp.where(j < lead, 0, 1 + div(j - lead, GROUP))
        return sbsem.at[jnp.where(e < mid, l * groups + g, EARLY * groups + l - EARLY)]

    def sb_mid(f):
        return sbsem.at[EARLY * groups + EARLY + div(f, chunks)]

    def send(src, dst, ssem, rsem_, t, s, r):
        pltpu.make_async_remote_copy(
            src_ref=src, dst_ref=dst, send_sem=ssem, recv_sem=rsem_,
            device_id={"tp": t, "side": s, "rep": r}, device_id_type=MESH,
        ).start()

    def wait(ref, sem):
        pltpu.make_async_copy(ref, ref, sem).wait()

    def run(fn, lo, hi):
        def body(c, _):
            fn(c)
            return 0

        lax.fori_loop(lo, hi, body, 0)

    def piece_rows(t, b, j):
        return pl.ds(pl.multiple_of(t * my_rows + b * BLOCK + j * PIECE, PIECE), PIECE)

    def sb_wait(c0, width, sem):
        wait(wbuf.at[pl.ds(c0, width), :, :, 1 - k], sem)

    def load_group(c0, g, slot):
        def load(j):
            pltpu.make_async_copy(wbuf.at[c0 + j], wv.at[slot, j], fsem.at[slot]).start()

        for j in range(lead):
            load(j)

        @pl.when(g > 0)
        def _():
            for j in range(lead, GROUP):
                load(j)

    def wait_group(g, slot):
        @pl.when(g == 0)
        def _():
            wait(wv.at[slot, pl.ds(0, lead)], fsem.at[slot])

        @pl.when(g > 0)
        def _():
            wait(wv.at[slot], fsem.at[slot])

    def width_of(g):
        return jnp.where(g == 0, lead, GROUP)

    def first_of(l, g):
        return l * chunks + jnp.where(g == 0, 0, lead + (g - 1) * GROUP)

    def matmuls(slot, rows, width):
        def weight(j, m):
            return wv[slot, j, m].reshape(d, UNIT)

        acts = []
        for j in range(width):
            a = lax.dot_general(weight(j, 0), rows, (((0,), (0,)), ((), ())), preferred_element_type=jnp.float32)
            acts.append(gelu(a).astype(jnp.bfloat16))
        down = jnp.concatenate([weight(j, 1) for j in range(width)], axis=1)
        return jnp.dot(down, jnp.concatenate(acts, axis=0), preferred_element_type=jnp.float32)

    def group_part(slot, g, hb, pb):
        @pl.when(g == 0)
        def _():
            p[pb] = matmuls(slot, h[hb], lead)

        @pl.when((g > 0) & (g < groups - 1))
        def _():
            p[pb] = p[pb] + matmuls(slot, h[hb], GROUP)

        @pl.when(g == groups - 1)
        def _():
            s = p[pb] + matmuls(slot, h[hb], GROUP)
            h[hb] = (h[hb].astype(jnp.float32) + s).astype(jnp.bfloat16)

    parts = ((w_up, g_up, nu), (w_dn, g_dn, nd))
    steps = gen + mid

    def chunk_at(s):
        return jnp.where(mod(s, 3) == 2, mid + div(s, 3), chunk_of(2 * div(s, 3) + mod(s, 3)))

    def cols_of(c):
        return div(c, chunks), pl.ds(pl.multiple_of(mod(c, chunks) * UNIT, UNIT), UNIT)

    def loads(s):
        l, cols = cols_of(chunk_at(s))
        slot = mod(s, LOAD_SLOTS)
        for m in range(2):
            for i, r in enumerate(parts[m][:2]):
                pltpu.make_async_copy(r.at[l, :, cols], fin.at[slot, 2 * m + i], lsem.at[slot]).start()

    def cast(s):
        slot, lslot = mod(s, STAGE_SLOTS), mod(s, LOAD_SLOTS)
        wait(fin.at[lslot], lsem.at[lslot])
        rate = rate_ref[0]
        for m in range(2):
            new = fin[lslot, 2 * m] - rate * fin[lslot, 2 * m + 1]
            fnew[lslot, m] = new
            stage[slot, m] = new.astype(jnp.bfloat16)

    @pl.when(side == 0)
    def _():
        for s in range(LOAD_SLOTS):
            loads(s)
        cast(0)

    barrier = pltpu.get_barrier_semaphore()
    peers = [(tp, 1 - side, rep)] + [
        (t, side, r) for t, r in ((flip_tp, rep), (tp, flip_rep), (flip_tp, flip_rep), (tp, sib_rep))
    ]
    for t, s_, r in peers:
        pl.semaphore_signal(
            barrier, inc=1, device_id={"tp": t, "side": s_, "rep": r}, device_id_type=MESH
        )
    pl.semaphore_wait(barrier, len(peers))

    @pl.when(side == 0)
    def _():
        def stores(s):
            l, cols = cols_of(chunk_at(s))
            slot = mod(s, LOAD_SLOTS)
            for m in range(2):
                pltpu.make_async_copy(fnew.at[slot, m], parts[m][2].at[l, :, cols], stsem.at[slot]).start()

        def wait_stored(s):
            slot = mod(s, LOAD_SLOTS)
            wait(fnew.at[slot], stsem.at[slot])

        def own_copy(s):
            slot = s % STAGE_SLOTS
            return pltpu.make_async_copy(stage.at[slot], both(chunk_at(s), own), csem.at[slot])

        def gathered_too(s):
            e = 2 * (s // 3) + s % 3
            return (s % 3 != 2) & (e >= mid) & (e < mid + chunks)

        def post(s):
            slot = s % STAGE_SLOTS
            src = stage.at[slot]
            stores(s)

            @pl.when(s % 3 != 2)
            def _():
                e = 2 * (s // 3) + s % 3
                c = chunk_of(e)
                send(src, both(c, own), tss.at[slot, 0], ysem.at[e], tp, 1, rep)

                @pl.when(gathered_too(s))
                def _():
                    own_copy(s).start()

                @pl.when(relayed(e))
                def _():
                    send(src, both(c, own), tss.at[slot, 1], rlsem.at[relay_index(e)], flip_tp, 0, flip_rep)

                @pl.when(e >= RELAY_LAG)
                def _():
                    relay(e - RELAY_LAG)

            @pl.when(s % 3 == 2)
            def _():
                f = div(s, 3)
                c = mid + f
                own_copy(s).start()
                send(src, both(c, own), tss.at[slot, 0], zsem(f), flip_tp, 0, rep)
                send(src, both(c, own), tss.at[slot, 1], xsem(f), tp, 0, flip_rep)

        def relay(e):
            @pl.when(relayed(e))
            def _():
                c = chunk_of(e)
                sem = rlsem.at[relay_index(e)]
                wait(both(c, dia), sem)
                send(both(c, dia), both(c, dia), ss.at[0, div(e, chunks)], sem, tp, 1, rep)

        def wait_sent(s):
            slot = s % STAGE_SLOTS
            is_mid = s % 3 == 2
            wait(stage.at[slot], tss.at[slot, 0])

            @pl.when(is_mid | relayed(2 * (s // 3) + s % 3))
            def _():
                wait(stage.at[slot], tss.at[slot, 1])

        def own_stage(f):
            c = mid + f
            send(both(c, own), both(c, own), ss.at[1, 0], zsem(f), flip_tp, 0, rep)
            send(both(c, own), both(c, own), ss.at[1, 1], xsem(f), tp, 0, flip_rep)

        def n_stage(f):
            c = mid + f
            wait(both(c, znb), zsem(f))
            wait(both(c, xnb), xsem(f))

            @pl.when(mod(f, 2) == 0)
            def _():
                send(both(c, znb), both(c, znb), ss.at[2, div(f, chunks)], dsem(f), tp, 0, flip_rep)

            @pl.when(mod(f, 2) == 1)
            def _():
                send(both(c, xnb), both(c, xnb), ss.at[3, div(f, chunks)], dsem(f), flip_tp, 0, rep)

        def d_stage(f):
            c = mid + f
            wait(both(c, dia), dsem(f))

            @pl.when(f < mid)
            def _():
                own_copy(3 * f + 2).wait()

            send(core_half(c, k), core_half(c, k), ss.at[4, div(f, chunks)], sb_mid(f), tp, 0, sib_rep)

        def body(s, _):
            @pl.when(s + LOAD_SLOTS - 1 < steps)
            def _():
                loads(s + LOAD_SLOTS - 1)

            @pl.when(s >= STAGE_SLOTS)
            def _():
                wait_sent(s - STAGE_SLOTS)

                @pl.when(gathered_too(s - STAGE_SLOTS))
                def _():
                    own_copy(s - STAGE_SLOTS).wait()

            @pl.when(s >= LOAD_SLOTS)
            def _():
                wait_stored(s - LOAD_SLOTS)

            cast(s)
            @pl.when(s >= 2)
            def _():
                post(s - 1)

            @pl.when(s % 3 == 2)
            def _():
                f = s // 3

                @pl.when(f >= N_LAG)
                def _():
                    n_stage(f - N_LAG)

                @pl.when(f >= D_LAG)
                def _():
                    d_stage(f - D_LAG)

            return 0

        post(0)
        lax.fori_loop(1, steps, body, 0)
        post(steps - 1)
        run(relay, gen - RELAY_LAG, gen)
        run(n_stage, mid - N_LAG, mid)
        run(d_stage, mid - D_LAG, mid)
        for s in range(steps - LOAD_SLOTS, steps):
            wait_stored(s)
        for s in range(steps - STAGE_SLOTS, steps):
            if s % 3 != 2 and mid <= 2 * (s // 3) + s % 3 < mid + chunks:
                own_copy(s).wait()
        for l in range(EARLY):
            sb_wait(mid + l * chunks, chunks, sb_mid(l * chunks))

        load_group(mid, 0, 0)
        per_block = EARLY * groups
        few = (blocks - MORE) * per_block
        n_visits = few + MORE * (per_block + groups)

        def place(t):
            u = t - few
            more = jnp.where(u >= per_block + groups, 1, 0)
            b = jnp.where(t < few, div(t, per_block), blocks - MORE + more)
            return b, jnp.where(t < few, mod(t, per_block), u - more * (per_block + groups))

        def give_back(b):
            send(h.at[b], h.at[blocks + b], hs.at[b], hr.at[b], tp, 1, rep)

        def visit(t, _):
            b, q = place(t)
            g, slot = mod(q, groups), mod(q, 2)
            wait_group(g, slot)

            for fn, after in ((own_stage, 0), (n_stage, 8), (d_stage, 18)):

                @pl.when((t >= after) & (t < after + chunks))
                def _():
                    fn(mid + t - after)

            @pl.when(t == few)
            def _():
                sb_wait(2 * mid, chunks, sb_mid(mid))

            @pl.when(t + 1 < n_visits)
            def _():
                _, nq = place(t + 1)
                ng = mod(nq, groups)
                load_group(first_of(EARLY + div(nq, groups), ng), ng, 1 - slot)

            @pl.when(q == 0)
            def _():
                @pl.when(b > 0)
                def _():
                    give_back(b - 1)

                wait(h.at[b], hr.at[b])

            group_part(slot, g, b, 0)
            return 0

        lax.fori_loop(0, n_visits, visit, 0)
        run(lambda b: wait(h.at[b], hs.at[b]), 0, blocks - 2)
        give_back(blocks - 1)

        def relay_out(i, _):
            @pl.when(i < n_relay)
            def _():
                wait(rin.at[i], rsem.at[0, i])
                send(rin.at[i], rx.at[i], psem.at[0, 0], rsem.at[1, i], flip_tp, 0, rep)

            @pl.when(i >= 1)
            def _():
                q = i - 1
                wait(rx.at[q], rsem.at[1, q])
                b, j, first = 0, 0, 0
                for rb, n in RELAYED:
                    b = jnp.where(q >= first, rb, b)
                    j = jnp.where(q >= first, q - first, j)
                    first += n
                send(rx.at[q], out.at[piece_rows(flip_tp, b, j)], psem.at[0, 1], osem.at[0], tp, 1, rep)

            return 0

        lax.fori_loop(0, n_relay + 1, relay_out, 0)
        wait(rin, psem.at[0, 0])
        wait(rx, psem.at[0, 1])
        run(wait_sent, steps - STAGE_SLOTS, steps)
        run(lambda b: wait(h.at[b], hs.at[b]), blocks - 2, blocks)
        for l in range(2 * EARLY):
            n = count(l * chunks, (l + 1) * chunks, relayed)
            if n:
                wait(wbuf.at[pl.ds(0, n), :, 0, 0, 0], ss.at[0, l])
        for i in range(2):
            wait(wbuf.at[pl.ds(0, chunks), :, 0, 0, 0], ss.at[1, i])
        for l in range(EARLY + 1):
            for m in range(2):
                n = count(l * chunks, (l + 1) * chunks, lambda f: f % 2 == m)
                wait(wbuf.at[pl.ds(0, n), :, 0, 0, 0], ss.at[2 + m, l])
            wait(wbuf.at[pl.ds(0, chunks), :, :, 0], ss.at[4, l])

    @pl.when(side == 1)
    def _():
        def y_stage(e):
            c, l = chunk_of(e), div(e, chunks)
            wait(both(c, own), ysem.at[e])
            send(both(c, own), both(c, own), ss.at[0, l], zsem(e), flip_tp, 1, rep)
            send(both(c, own), both(c, own), ss.at[1, l], xsem(e), tp, 1, flip_rep)

        def n_stage(e):
            c, l = chunk_of(e), div(e, chunks)
            wait(both(c, znb), zsem(e))
            wait(both(c, xnb), xsem(e))
            direct = jnp.logical_not(relayed(e))

            @pl.when(direct & jnp.logical_not(by_z(e)))
            def _():
                send(both(c, znb), both(c, znb), ss.at[2, l], dsem(e), tp, 1, flip_rep)

            @pl.when(direct & by_z(e))
            def _():
                send(both(c, xnb), both(c, xnb), ss.at[3, l], dsem(e), flip_tp, 1, rep)

        def d_stage(e):
            c = chunk_of(e)

            @pl.when(relayed(e))
            def _():
                wait(both(c, dia), rlsem.at[relay_index(e)])

            @pl.when(jnp.logical_not(relayed(e)))
            def _():
                wait(both(c, dia), dsem(e))

            send(core_half(c, k), core_half(c, k), ss.at[4, div(e, chunks)], sb_of(e), tp, 1, sib_rep)

        turn = EARLY * groups * blocks

        def front(i, t):
            a, s1, jump, s2 = FRONTS[i]
            late = 16 * jump + s1 * turn + s2 * (t - turn)
            return jnp.minimum(gen, a + (jnp.where(t <= turn, s1 * t, late) >> 4))

        def pload(b):
            rows = pl.ds(pl.multiple_of(tp * my_rows + b * BLOCK, BLOCK), BLOCK)
            return pltpu.make_async_copy(prompts.at[rows], rows_buf.at[b % 2], iosem.at[b % 2])

        pload(0).start()
        for b in range(blocks):
            if b + 1 < blocks:
                pload(b + 1).start()
            pload(b).wait()
            for j in range(pieces):
                h[b, :, pl.ds(j * PIECE, PIECE)] = rows_buf[b % 2, pl.ds(j * PIECE, PIECE), :].T

        n_pro = FRONTS[0][0]
        for e in range(n_pro):
            y_stage(e)
            for i, fn in ((1, n_stage), (2, d_stage)):
                if e >= n_pro - FRONTS[i][0]:
                    fn(e - (n_pro - FRONTS[i][0]))
        sb_wait(0, lead, sbsem.at[0])
        load_group(0, 0, 0)

        def put(b, j):
            src = rows_buf.at[mod(b, 2), pl.ds(j * PIECE, PIECE), :]
            rows = piece_rows(tp, b, j)
            pltpu.make_async_copy(src, out.at[rows], psem.at[mod(b, 2), 0]).start()
            n, i, first = 0, 0, 0
            for rb, m in RELAYED:
                n = jnp.where(b == rb, m, n)
                i = jnp.where(b == rb, first + min(j, m - 1), i)
                first += m

            @pl.when(j < n)
            def _():
                send(src, rin.at[i], psem.at[mod(b, 2), 1], rsem.at[0, i], tp, 0, rep)

            @pl.when(j >= n)
            def _():
                send(src, out.at[rows], psem.at[mod(b, 2), 1], osem.at[0], flip_tp, 1, rep)

        def put_wait(b):
            for i in range(2):
                wait(rows_buf.at[mod(b, 2)], psem.at[mod(b, 2), i])

        n_rest = groups - 1
        wide = turn - n_rest * blocks
        n_first = blocks - MORE
        n_tasks = n_first + blocks
        first_late, last_late = 2 * EARLY, 2 * EARLY + 1

        def late_task(q):
            u = q - 2 * FIRST_LATE
            each = (u >= 0) & (u < 2 * (n_first - FIRST_LATE))
            first = (q < FIRST_LATE) | (each & ((u & 1) == 0))
            b = jnp.where(q < FIRST_LATE, q, jnp.where(u < 0, q - FIRST_LATE, jnp.where(each, FIRST_LATE + (u >> 1), q - n_first)))
            return jnp.where(first, first_late, last_late), b

        def rest(t):
            u = t - wide
            b = (u * (128 // n_rest + 1)) >> 7
            return b, 1 + u - n_rest * b

        def give(b):
            send(h.at[b], h.at[b], hs.at[b], hr.at[b], tp, 0, rep)

        def forward(t):
            for i, fn in enumerate((y_stage, n_stage, d_stage)):
                run(fn, front(i, t), front(i, t + 1))

        def early_visit(t, _):
            split = t >= wide
            rb, rg = rest(t)
            l = jnp.where(split, EARLY - 1, div(t, groups * blocks))
            g = jnp.where(split, rg, mod(div(t, blocks), groups))
            b = jnp.where(split, rb, mod(t, blocks))
            slot = mod(jnp.where(split, t - wide + 1, div(t, blocks)), 2)

            @pl.when(split | (b == 0))
            def _():
                wait_group(g, slot)

            forward(t)

            @pl.when((t > wide) & (rg == 1))
            def _():
                give(rb - 1)

            @pl.when((t < wide) & (b == blocks // 2))
            def _():
                c0 = first_of(l, g) + width_of(g)
                ng = mod(g + 1, groups)
                sem = sb_of(c0)

                @pl.when(ng == 0)
                def _():
                    sb_wait(c0, lead, sem)

                @pl.when(ng > 0)
                def _():
                    sb_wait(c0, GROUP, sem)

                load_group(c0, ng, 1 - slot)

            @pl.when(t == wide)
            def _():
                for g_ in range(2, groups):
                    c0 = (EARLY - 1) * chunks + lead + (g_ - 1) * GROUP
                    sb_wait(c0, GROUP, sb_of(c0))

            @pl.when(split & (t + 1 < turn))
            def _():
                _, ng = rest(t + 1)
                load_group(first_of(EARLY - 1, ng), ng, 1 - slot)

            @pl.when(t == turn - 1)
            def _():
                sb_wait(2 * mid, chunks, sb_of(mid))
                load_group(2 * mid, 0, 1 - slot)

            group_part(slot, g, b, b)
            return 0

        def late_visit(u, _):
            l, b = late_task(div(u, groups))
            g = mod(u, groups)
            slot = mod(u + n_rest * blocks + 1, 2)
            hb = blocks + b
            wait_group(g, slot)

            @pl.when(u < FIRST_LATE * groups)
            def _():
                forward(turn + u)

                @pl.when(u == 0)
                def _():
                    give(blocks - 1)

                @pl.when(u == FIRST_LATE * groups - 1)
                def _():
                    for i, fn in enumerate((y_stage, n_stage, d_stage)):
                        run(fn, front(i, turn + u + 1), gen)
                    sb_wait(2 * mid + chunks, chunks, sb_of(mid + chunks))

            @pl.when(u + 1 < n_tasks * groups)
            def _():
                nl, _ = late_task(div(u + 1, groups))
                ng = mod(u + 1, groups)
                load_group(first_of(nl, ng), ng, 1 - slot)

            @pl.when((g == 0) & ((l == first_late) | (b >= n_first)))
            def _():
                wait(h.at[hb], hr.at[b])

            group_part(slot, g, hb, b)

            @pl.when((l == last_late) & (g == groups - 1))
            def _():
                @pl.when(b >= 2)
                def _():
                    put_wait(b - 2)

                for j in range(pieces):
                    cols = pl.ds(j * PIECE, PIECE)
                    rows_buf[mod(b, 2), cols, :] = h[hb, :, cols].T
                    if j >= 1:
                        put(b, j - 1)
                put(b, pieces - 1)

            return 0

        lax.fori_loop(0, turn, early_visit, 0)
        lax.fori_loop(0, (n_tasks - 1) * groups, late_visit, 0)

        b, hb, half = blocks - 1, 2 * blocks - 1, BLOCK // 2
        wait(h.at[hb], hr.at[b])
        put_wait(b - 2)

        def half_visits(i, _):
            cols = pl.ds(pl.multiple_of(i * half, half), half)
            for g in range(groups):
                slot = ((n_tasks - 1) * groups + n_rest * blocks + 1 + g) % 2
                wait_group(g, slot)
                if g + 1 < groups:
                    load_group(first_of(last_late, g + 1), g + 1, 1 - slot)
                else:

                    @pl.when(i == 0)
                    def _():
                        load_group(first_of(last_late, 0), 0, 1 - slot)

                rows = h[hb, :, cols]
                t = matmuls(slot, rows, GROUP if g else lead)
                if g:
                    t = p[b, :, cols] + t
                if g + 1 < groups:
                    p[b, :, cols] = t
                else:
                    t = (rows.astype(jnp.float32) + t).astype(jnp.bfloat16)
                    for j in range(half // PIECE):
                        at = pl.multiple_of(i * half + j * PIECE, PIECE)
                        rows_buf[b % 2, pl.ds(at, PIECE), :] = t[:, j * PIECE : (j + 1) * PIECE].T
            for j in range(half // PIECE):
                at = i * half + j * PIECE
                src = rows_buf.at[b % 2, pl.ds(pl.multiple_of(at, PIECE), PIECE), :]
                to = pl.ds(pl.multiple_of(tp * my_rows + b * BLOCK + at, PIECE), PIECE)
                pltpu.make_async_copy(src, out.at[to], psem.at[b % 2, 0]).start()
                send(src, out.at[to], psem.at[b % 2, 1], osem.at[0], flip_tp, 1, rep)
            return 0

        lax.fori_loop(0, 2, half_visits, 0)
        for b in range(blocks - 2, blocks):
            put_wait(b)
        run(lambda b: wait(h.at[b], hs.at[b]), 0, blocks)
        wait(out.at[pl.ds(pl.multiple_of(flip_tp * my_rows, BLOCK), my_rows)], osem.at[0])
        for l in range(2 * EARLY):
            for i in range(5):
                if i == 4:
                    wait(wbuf.at[pl.ds(0, chunks), :, :, 0], ss.at[i, l])
                else:
                    kinds = (None, None, lambda e: not relayed(e) and not by_z(e), lambda e: not relayed(e) and by_z(e))
                    n = chunks if i < 2 else count(l * chunks, (l + 1) * chunks, kinds[i])
                    wait(wbuf.at[pl.ds(0, n), :, 0, 0, 0], ss.at[i, l])


def finish_kernel(up, dn, rows, new_up, new_dn, out, buf, zbuf, lsem, ssem, zsem):
    layers = up.shape[0]
    n_rows = rows.shape[0]
    slots, band, hidden = buf.shape
    side = lax.axis_index("side")
    items = [(i, o, l) for l in range(layers) for i, o in ((up, new_up), (dn, new_dn))]
    piece = zbuf.shape[1]
    n_pieces = n_rows // piece
    n_slots = zbuf.shape[0]

    def pipeline(n, n_slots, load, store, zeros):
        for i in range(min(n_slots, n)):
            load(i).start()
        half = n_slots // 2
        done = 0
        for i in range(n):
            load(i).wait()
            store(i).start()
            upto = len(zeros) * (i + 1) // n
            for cp in zeros[done:upto]:
                cp.start()
            done = upto
            nxt = i + half
            if i >= half and nxt < n:
                store(nxt - n_slots).wait()
                load(nxt).start()
        for i in range(max(n - n_slots, 0), n):
            store(i).wait()
        for cp in zeros:
            cp.wait()

    @pl.when(side == 0)
    def _():
        zbuf[0] = jnp.zeros(zbuf.shape[1:], zbuf.dtype)
        zeros = [
            pltpu.make_async_copy(zbuf.at[0], out.at[pl.ds(i * piece, piece)], zsem.at[i]) for i in range(n_pieces)
        ]

        def load(i):
            src, _, l = items[i]
            return pltpu.make_async_copy(src.at[l], buf.at[i % slots], lsem.at[i % slots])

        def store(i):
            _, dst, l = items[i]
            return pltpu.make_async_copy(buf.at[i % slots], dst.at[l], ssem.at[i % slots])

        pipeline(len(items), slots, load, store, zeros)

    @pl.when(side == 1)
    def _():
        buf[0] = jnp.zeros(buf.shape[1:], buf.dtype)
        zeros = [pltpu.make_async_copy(buf.at[0], dst.at[l], zsem.at[i]) for i, (_, dst, l) in enumerate(items)]

        def load(i):
            return pltpu.make_async_copy(rows.at[pl.ds(i * piece, piece)], zbuf.at[i % n_slots], lsem.at[i % n_slots])

        def store(i):
            return pltpu.make_async_copy(zbuf.at[i % n_slots], out.at[pl.ds(i * piece, piece)], ssem.at[i % n_slots])

        pipeline(n_pieces, n_slots, load, store, zeros)


def solution(mesh):
    up_spec = P("side", None, ("rep", "tp"), None)
    down_spec = P("side", None, None, ("rep", "tp"))
    tok_spec = P("side", "rep", None, None)

    def device_step(w_up, w_down, g_up, g_down, learn_rate, prompts):
        layers, band, hidden = w_up.shape[1:]
        n_rows, d = prompts.shape[2:]
        chunks = hidden // UNIT
        total = layers * chunks
        my_rows = n_rows // 2
        blocks, pieces = my_rows // BLOCK, BLOCK // PIECE
        weights = (w_up[0], jnp.swapaxes(w_down[0], 1, 2), g_up[0], jnp.swapaxes(g_down[0], 1, 2))
        smem = pl.BlockSpec(memory_space=pltpu.SMEM)
        hbm = pl.BlockSpec(memory_space=pl.ANY)
        bf16 = jnp.bfloat16
        relay = jax.ShapeDtypeStruct((sum(n for _, n in RELAYED), PIECE, d), bf16)
        new_w = jax.ShapeDtypeStruct((layers, band, hidden), jnp.float32)
        rows = jax.ShapeDtypeStruct((n_rows, d), bf16)
        rows_mid, up_mid, dn_mid, _, _, _ = pl.pallas_call(
            sync_kernel,
            name="sync_and_forward",
            out_shape=(
                rows,
                new_w,
                new_w,
                jax.ShapeDtypeStruct((total, 2, 2, 2, 2, band, UNIT), bf16),
                relay,
                relay,
            ),
            in_specs=[smem] + [hbm] * 5,
            out_specs=(hbm,) * 6,
            scratch_shapes=[
                pltpu.VMEM((2 * blocks, d, BLOCK), bf16),
                pltpu.VMEM((blocks, d, BLOCK), jnp.float32),
                pltpu.VMEM((2, GROUP, 2, 2, 2, 2, band, UNIT), bf16),
                pltpu.VMEM((LOAD_SLOTS, 4, band, UNIT), jnp.float32),
                pltpu.VMEM((LOAD_SLOTS, 2, band, UNIT), jnp.float32),
                pltpu.VMEM((STAGE_SLOTS, 2, band, UNIT), bf16),
                pltpu.VMEM((2, BLOCK, d), bf16),
                pltpu.SemaphoreType.DMA((2 * EARLY * chunks,)),
                pltpu.SemaphoreType.DMA((3, RING)),
                pltpu.SemaphoreType.DMA((EARLY * chunks // 6 + chunks // 3 + 1,)),
                pltpu.SemaphoreType.DMA((EARLY * (-(-chunks // GROUP)) + 2 * EARLY + 1,)),
                pltpu.SemaphoreType.DMA((5, 2 * EARLY)),
                pltpu.SemaphoreType.DMA((LOAD_SLOTS,)),
                pltpu.SemaphoreType.DMA((LOAD_SLOTS,)),
                pltpu.SemaphoreType.DMA((2,)),
                pltpu.SemaphoreType.DMA((STAGE_SLOTS, 2)),
                pltpu.SemaphoreType.DMA((STAGE_SLOTS,)),
                pltpu.SemaphoreType.DMA((2,)),
                pltpu.SemaphoreType.DMA((2, 2)),
                pltpu.SemaphoreType.DMA((1,)),
                pltpu.SemaphoreType.DMA((2, sum(n for _, n in RELAYED))),
                pltpu.SemaphoreType.DMA((blocks,)),
                pltpu.SemaphoreType.DMA((blocks,)),
            ],
            compiler_params=pltpu.CompilerParams(
                collective_id=0, has_side_effects=True, vmem_limit_bytes=60 * 1024 * 1024
            ),
        )(learn_rate, *weights, prompts[0, 0])
        new_up, new_dn, gen_out = pl.pallas_call(
            finish_kernel,
            name="write_outputs",
            out_shape=(new_w, new_w, rows),
            in_specs=[hbm] * 3,
            out_specs=(hbm,) * 3,
            scratch_shapes=[
                pltpu.VMEM((8, band, hidden), jnp.float32),
                pltpu.VMEM((8, n_rows // 16, d), bf16),
                pltpu.SemaphoreType.DMA((8,)),
                pltpu.SemaphoreType.DMA((8,)),
                pltpu.SemaphoreType.DMA((max(16, 2 * layers),)),
            ],
            compiler_params=pltpu.CompilerParams(vmem_limit_bytes=62 * 1024 * 1024),
        )(up_mid, dn_mid, rows_mid)
        return new_up[None], jnp.swapaxes(new_dn, 1, 2)[None], gen_out[None, None]

    return jax.shard_map(
        device_step,
        mesh=mesh,
        in_specs=(up_spec, down_spec, up_spec, down_spec, P("side"), tok_spec),
        out_specs=(up_spec, down_spec, tok_spec),
        check_vma=False,
    )
```

profile of v0, /device:TPU:0, one launch (start us, length us, event | category | flops | bytes accessed | tf_op | source)
XLA Modules:
  0.0 457.0 jit_solution(11641950252148075015)
XLA Ops:
  1.3 432.4 %sync_and_forward.1 = (bf16[8192,896]{1,0:T(8,128)(2,1)}, f32[6,112,4864]{2,1,0:T(8,128)}, f32[6,112,4864]{2,1,0:T(8,128)}, bf16[114,2,2,2,2,112,256]{6,5,4,3,2,...) custom-call(f32[1]{0:T(128)S(6)} %copy.9.rate_ref, f32[6,112,4864]{2,1,0:T(8,128)} %bitcast.15, ...), custom_call_target="tpu_custom_call" | custom-call | tf_op jit(solution)/shard_map/sync_and_forward/pallas_call | solution.py:804
  433.7 23.1 %write_outputs.1 = (f32[6,112,4864]{2,1,0:T(8,128)}, f32[6,112,4864]{2,1,0:T(8,128)}, bf16[8192,896]{1,0:T(8,128)(2,1)}) custom-call(f32[6,112,4864]{2,1,0:T(8,128)} %get-tuple-element.9.up, f32[6,112,4864]{2,1,0:T(8,128)} %get-tuple-element.10.dn, bf16[8192,896]{1,0:T(8,128)(2,1)} %get-tuple-element.11.rows), custom_call_target="tpu_custom_call" | custom-call | tf_op jit(solution)/shard_map/write_outputs/pallas_call | solution.py:846
where the time goes:
time: 466 us; the launch traced here: 457 us
  Pallas kernels  456 us (98%)
    pallas_call x1, Pallas kernels, device_step(): pl.pallas_call(sync_kernel, name='sync_and_forward', out_shape=(rows, new...  432 us
    pallas_call x1, Pallas kernels, device_step(): pl.pallas_call(finish_kernel, name='write_outputs', out_shape=(new_w, new...  23.1 us

commit v1 on v0

--- a/solution.py
+++ b/solution.py
@@ -157,10 +157,11 @@
     def first_of(l, g):
         return l * chunks + jnp.where(g == 0, 0, lead + (g - 1) * GROUP)
 
-    def matmuls(slot, rows, width):
+    def matmuls(slot, hb, width):
         def weight(j, m):
             return wv[slot, j, m].reshape(d, UNIT)
 
+        rows = h[hb]
         acts = []
         for j in range(width):
             a = lax.dot_general(weight(j, 0), rows, (((0,), (0,)), ((), ())), preferred_element_type=jnp.float32)
@@ -171,15 +172,15 @@
     def group_part(slot, g, hb, pb):
         @pl.when(g == 0)
         def _():
-            p[pb] = matmuls(slot, h[hb], lead)
+            p[pb] = matmuls(slot, hb, lead)
 
         @pl.when((g > 0) & (g < groups - 1))
         def _():
-            p[pb] = p[pb] + matmuls(slot, h[hb], GROUP)
+            p[pb] = p[pb] + matmuls(slot, hb, GROUP)
 
         @pl.when(g == groups - 1)
         def _():
-            s = p[pb] + matmuls(slot, h[hb], GROUP)
+            s = p[pb] + matmuls(slot, hb, GROUP)
             h[hb] = (h[hb].astype(jnp.float32) + s).astype(jnp.bfloat16)
 
     parts = ((w_up, g_up, nu), (w_dn, g_dn, nd))
@@ -667,45 +668,7 @@
             return 0
 
         lax.fori_loop(0, turn, early_visit, 0)
-        lax.fori_loop(0, (n_tasks - 1) * groups, late_visit, 0)
-
-        b, hb, half = blocks - 1, 2 * blocks - 1, BLOCK // 2
-        wait(h.at[hb], hr.at[b])
-        put_wait(b - 2)
-
-        def half_visits(i, _):
-            cols = pl.ds(pl.multiple_of(i * half, half), half)
-            for g in range(groups):
-                slot = ((n_tasks - 1) * groups + n_rest * blocks + 1 + g) % 2
-                wait_group(g, slot)
-                if g + 1 < groups:
-                    load_group(first_of(last_late, g + 1), g + 1, 1 - slot)
-                else:
-
-                    @pl.when(i == 0)
-                    def _():
-                        load_group(first_of(last_late, 0), 0, 1 - slot)
-
-                rows = h[hb, :, cols]
-                t = matmuls(slot, rows, GROUP if g else lead)
-                if g:
-                    t = p[b, :, cols] + t
-                if g + 1 < groups:
-                    p[b, :, cols] = t
-                else:
-                    t = (rows.astype(jnp.float32) + t).astype(jnp.bfloat16)
-                    for j in range(half // PIECE):
-                        at = pl.multiple_of(i * half + j * PIECE, PIECE)
-                        rows_buf[b % 2, pl.ds(at, PIECE), :] = t[:, j * PIECE : (j + 1) * PIECE].T
-            for j in range(half // PIECE):
-                at = i * half + j * PIECE
-                src = rows_buf.at[b % 2, pl.ds(pl.multiple_of(at, PIECE), PIECE), :]
-                to = pl.ds(pl.multiple_of(tp * my_rows + b * BLOCK + at, PIECE), PIECE)
-                pltpu.make_async_copy(src, out.at[to], psem.at[b % 2, 0]).start()
-                send(src, out.at[to], psem.at[b % 2, 1], osem.at[0], flip_tp, 1, rep)
-            return 0
-
-        lax.fori_loop(0, 2, half_visits, 0)
+        lax.fori_loop(0, n_tasks * groups, late_visit, 0)
         for b in range(blocks - 2, blocks):
             put_wait(b)
         run(lambda b: wait(h.at[b], hs.at[b]), 0, blocks)

time: 466 us -> 466 us (level)
  no operation moved by 1% of the time
where the time goes in v1:
time: 466 us; the launch traced here: 457 us
  Pallas kernels  456 us (98%)
    pallas_call x1, Pallas kernels, device_step(): pl.pallas_call(sync_kernel, name='sync_and_forward', out_shape=(rows, new...  432 us
    pallas_call x1, Pallas kernels, device_step(): pl.pallas_call(finish_kernel, name='write_outputs', out_shape=(new_w, new...  23.1 us

profile of v1, /device:TPU:0, one launch (start us, length us, event | category | flops | bytes accessed | tf_op | source)
XLA Modules:
  0.0 457.0 jit_solution(5000861060535200814)
XLA Ops:
  1.3 432.4 %sync_and_forward.1 = (bf16[8192,896]{1,0:T(8,128)(2,1)}, f32[6,112,4864]{2,1,0:T(8,128)}, f32[6,112,4864]{2,1,0:T(8,128)}, bf16[114,2,2,2,2,112,256]{6,5,4,3,2,...) custom-call(f32[1]{0:T(128)S(6)} %copy.9.rate_ref, f32[6,112,4864]{2,1,0:T(8,128)} %bitcast.15, ...), custom_call_target="tpu_custom_call" | custom-call | tf_op jit(solution)/shard_map/sync_and_forward/pallas_call | solution.py:767
  433.7 23.1 %write_outputs.1 = (f32[6,112,4864]{2,1,0:T(8,128)}, f32[6,112,4864]{2,1,0:T(8,128)}, bf16[8192,896]{1,0:T(8,128)(2,1)}) custom-call(f32[6,112,4864]{2,1,0:T(8,128)} %get-tuple-element.9.up, f32[6,112,4864]{2,1,0:T(8,128)} %get-tuple-element.10.dn, bf16[8192,896]{1,0:T(8,128)(2,1)} %get-tuple-element.11.rows), custom_call_target="tpu_custom_call" | custom-call | tf_op jit(solution)/shard_map/write_outputs/pallas_call | solution.py:809

commit v2 on v1

--- a/solution.py
+++ b/solution.py
@@ -16,7 +16,7 @@
 RING = 32
 N_LAG, D_LAG = 3, 6
 RELAY_LAG = 4
-FIRST_LATE = 3
+FIRST_LATE = 2
 MORE = 2
 RELAYED = ((5, 2), (6, 2))
 FRONTS = ((10, 15, 1, 40), (8, 14, 1, 44), (6, 13, 3, 24))

time: 466 us -> 463 us (level); the launches traced: 457 us -> 461 us
  no operation moved by 1% of the time
where the time goes in v2:
time: 463 us; the launch traced here: 461 us
  Pallas kernels  460 us (99%)
    pallas_call x1, Pallas kernels, device_step(): pl.pallas_call(sync_kernel, name='sync_and_forward', out_shape=(rows, new...  437 us
    pallas_call x1, Pallas kernels, device_step(): pl.pallas_call(finish_kernel, name='write_outputs', out_shape=(new_w, new...  23.1 us

profile of v2, /device:TPU:0, one launch (start us, length us, event | category | flops | bytes accessed | tf_op | source)
XLA Modules:
  0.0 461.2 jit_solution(1957716534928765678)
XLA Ops:
  1.3 436.6 %sync_and_forward.1 = (bf16[8192,896]{1,0:T(8,128)(2,1)}, f32[6,112,4864]{2,1,0:T(8,128)}, f32[6,112,4864]{2,1,0:T(8,128)}, bf16[114,2,2,2,2,112,256]{6,5,4,3,2,...) custom-call(f32[1]{0:T(128)S(6)} %copy.9.rate_ref, f32[6,112,4864]{2,1,0:T(8,128)} %bitcast.15, ...), custom_call_target="tpu_custom_call" | custom-call | tf_op jit(solution)/shard_map/sync_and_forward/pallas_call | solution.py:767
  437.9 23.1 %write_outputs.1 = (f32[6,112,4864]{2,1,0:T(8,128)}, f32[6,112,4864]{2,1,0:T(8,128)}, bf16[8192,896]{1,0:T(8,128)(2,1)}) custom-call(f32[6,112,4864]{2,1,0:T(8,128)} %get-tuple-element.9.up, f32[6,112,4864]{2,1,0:T(8,128)} %get-tuple-element.10.dn, bf16[8192,896]{1,0:T(8,128)(2,1)} %get-tuple-element.11.rows), custom_call_target="tpu_custom_call" | custom-call | tf_op jit(solution)/shard_map/write_outputs/pallas_call | solution.py:809

commit v3 on v2

--- a/solution.py
+++ b/solution.py
@@ -12,8 +12,8 @@
 PIECE = 128
 EARLY = 2
 LOAD_SLOTS = 4
-STAGE_SLOTS = 36
-RING = 32
+STAGE_SLOTS = 32
+RING = 24
 N_LAG, D_LAG = 3, 6
 RELAY_LAG = 4
 FIRST_LATE = 2

time: 463 us -> 463 us (level)
  no operation moved by 1% of the time
where the time goes in v3:
time: 463 us; the launch traced here: 461 us
  Pallas kernels  459 us (99%)
    pallas_call x1, Pallas kernels, device_step(): pl.pallas_call(sync_kernel, name='sync_and_forward', out_shape=(rows, new...  436 us
    pallas_call x1, Pallas kernels, device_step(): pl.pallas_call(finish_kernel, name='write_outputs', out_shape=(new_w, new...  23.1 us

profile of v3, /device:TPU:0, one launch (start us, length us, event | category | flops | bytes accessed | tf_op | source)
XLA Modules:
  0.0 460.8 jit_solution(3760054313260429088)
XLA Ops:
  1.3 436.2 %sync_and_forward.1 = (bf16[8192,896]{1,0:T(8,128)(2,1)}, f32[6,112,4864]{2,1,0:T(8,128)}, f32[6,112,4864]{2,1,0:T(8,128)}, bf16[114,2,2,2,2,112,256]{6,5,4,3,2,...) custom-call(f32[1]{0:T(128)S(6)} %copy.9.rate_ref, f32[6,112,4864]{2,1,0:T(8,128)} %bitcast.15, ...), custom_call_target="tpu_custom_call" | custom-call | tf_op jit(solution)/shard_map/sync_and_forward/pallas_call | solution.py:767
  437.5 23.1 %write_outputs.1 = (f32[6,112,4864]{2,1,0:T(8,128)}, f32[6,112,4864]{2,1,0:T(8,128)}, bf16[8192,896]{1,0:T(8,128)(2,1)}) custom-call(f32[6,112,4864]{2,1,0:T(8,128)} %get-tuple-element.9.up, f32[6,112,4864]{2,1,0:T(8,128)} %get-tuple-element.10.dn, bf16[8192,896]{1,0:T(8,128)(2,1)} %get-tuple-element.11.rows), custom_call_target="tpu_custom_call" | custom-call | tf_op jit(solution)/shard_map/write_outputs/pallas_call | solution.py:809
